TPU v7x, 512 devices: a whole 4x4x16 slice. The times are simulated.
512 devices in a mesh: group: 16 (over y, x), member: 32 (over z, core).
Axes of the slice: x: 4, y: 4, z: 16, core: 2. Of those that a mesh axis runs over, the one named last changes fastest.
Arguments:
- tokens: bfloat16 [65536, 2048], P(('group', 'member')), may hold values from -6 to 6
- cotangent: bfloat16 [65536, 2048], P(('group', 'member')), may hold values from -6 to 6
- w_gate: bfloat16 [2048, 512], P('member'), may hold values from -0.125 to 0.125
- w_up: bfloat16 [2048, 512], P('member'), may hold values from -0.125 to 0.125
- w_down: bfloat16 [2048, 512], P('member'), may hold values from -0.125 to 0.125
- basis: float32 [2048, 256], P('member'), may hold values from -0.088388348 to 0.088388348
- first_moment: float32 [3, 256, 512], P(None, 'member'), may hold values from -3 to 3
- second_moment: float32 [3, 256, 512], P(None, 'member'), may hold values from 0.1 to 2
Outputs:
- input_grad: bfloat16 [65536, 2048], P(('group', 'member'))
- new_first: float32 [3, 256, 512], P(None, 'member')
- new_second: float32 [3, 256, 512], P(None, 'member')
- updates: float32 [3, 2048, 512], P(None, 'member')
All inputs are finite; a program needn't handle non-finite values.
Results may differ from a plain program's by a relative error of at most 0.008.
Values may be sent and summed in bfloat16 or wider, within the bound.
A program may use at most 64 MiB of HBM per device.

v0:
```python
import math
import jax
import jax.numpy as jnp
from jax import lax
from jax.sharding import Mesh
from jax.sharding import PartitionSpec as P

FF = 512
RANK = 256
MEMBER = ("member_0", "member_1")
GROUP_MEMBER = ("group", "member_0", "member_1")


def in_one_piece(arrays, axis, dim, along):
    both = jnp.concatenate(arrays, axis=along)
    whole, at, gathered = (lax.all_gather(both, axis, axis=dim, tiled=True), 0, [])
    for a in arrays:
        gathered.append(lax.slice_in_dim(whole, at, at + a.shape[along], axis=along))
        at += a.shape[along]
    return tuple(gathered)


def joined_along(pieces, dim):
    pieces = jnp.moveaxis(pieces, 0, dim)
    shape = pieces.shape
    return pieces.reshape(*shape[:dim], shape[dim] * shape[dim + 1], *shape[dim + 2 :])


def copy_for_each(value, axis):
    peers = lax.axis_size(axis)
    return lax.all_to_all(
        jnp.broadcast_to(value[None], (peers, *value.shape)), axis, 0, 0, tiled=True
    )


def gathered_copies(value, axis, dim):
    return joined_along(copy_for_each(value, axis), dim)


def in_blocks(value, dim, peers):
    before, after = (value.shape[:dim], value.shape[dim + 1 :])
    return jnp.moveaxis(value.reshape(*before, peers, -1, *after), dim, 0)


def sum_at_owner(value, axis, dim):
    pieces = in_blocks(value, dim, lax.axis_size(axis))
    arrived = lax.all_to_all(pieces, axis, split_axis=0, concat_axis=0, tiled=True)
    return arrived.sum(axis=0)


def of_everyone(value, axis):
    return copy_for_each(value, axis).sum(axis=0)


def gather_in_order(value, axes, order):
    pieces = value[None]
    for k in order:
        pieces = lax.all_gather(pieces, axes[k], axis=0, tiled=True)
    block = [lax.axis_size(axes[k]) for k in reversed(order)]
    pieces = pieces.reshape(*block, *value.shape)
    turned = sorted(range(len(order)), key=lambda place: order[len(order) - 1 - place])
    return pieces.transpose(*turned, *range(len(order), pieces.ndim)).reshape(-1, *value.shape)


def whole_of(value, axes, order, dim):
    return joined_along(gather_in_order(value, axes, order), dim)


def contract_rows(left, right):
    return lax.dot_general(
        left, right, (((0,), (0,)), ((), ())), preferred_element_type=jnp.float32
    )


def contract_cols(left, right):
    return lax.dot_general(
        left, right, (((1,), (1,)), ((), ())), preferred_element_type=jnp.float32
    )


def split_parts(values):
    high_part = values.astype(jnp.bfloat16)
    low_part = (values - high_part.astype(jnp.float32)).astype(jnp.bfloat16)
    return (high_part, low_part)


def local(tokens, cotangent, w_gate, w_up, w_down, basis, first_moment, second_moment):
    full_gate, full_up, full_down = in_one_piece((w_gate, w_up, w_down), MEMBER, 0, 1)
    gate = jnp.dot(tokens, full_gate, preferred_element_type=jnp.float32)
    up = jnp.dot(tokens, full_up, preferred_element_type=jnp.float32)
    dhid = jnp.dot(cotangent, full_down, preferred_element_type=jnp.float32)
    sig = jax.nn.sigmoid(gate)
    silu = gate * sig
    hidden = (silu * up).astype(jnp.bfloat16)
    dgate = (dhid * up * sig * (1.0 + gate * (1.0 - sig))).astype(jnp.bfloat16)
    dup = (dhid * silu).astype(jnp.bfloat16)
    dx_full = contract_cols(dgate, full_gate) + contract_cols(dup, full_up)
    input_grad = dx_full.astype(jnp.bfloat16)
    full_basis = gathered_copies(basis, MEMBER, 0)
    highest = lax.Precision.HIGHEST
    basis_high, basis_low = split_parts(full_basis)
    x_proj = jnp.dot(tokens, basis_high, preferred_element_type=jnp.float32) + jnp.dot(
        tokens, basis_low, preferred_element_type=jnp.float32
    )
    y_proj = jnp.dot(cotangent, basis_high, preferred_element_type=jnp.float32) + jnp.dot(
        cotangent, basis_low, preferred_element_type=jnp.float32
    )
    x_high, x_low = split_parts(x_proj)
    y_high, y_low = split_parts(y_proj)
    low_gate = contract_rows(x_high, dgate) + contract_rows(x_low, dgate)
    low_up = contract_rows(x_high, dup) + contract_rows(x_low, dup)
    low_down = contract_rows(y_high, hidden) + contract_rows(y_low, hidden)
    local_low = jnp.stack([low_gate, low_up, low_down])
    partial_rows = sum_at_owner(local_low, MEMBER, 1)
    share = of_everyone(partial_rows, "group")
    squares = of_everyone(jnp.sum(share * share), MEMBER)
    limit = math.sqrt(3.0 * RANK * FF)
    factor = jnp.minimum(1.0, limit / jnp.sqrt(squares + 1e-06))
    grad_low = factor * share
    new_first = 0.5 * first_moment + 0.5 * grad_low
    new_second = 0.9 * second_moment + 0.1 * grad_low * grad_low
    step = (new_first / (jnp.sqrt(new_second) + 1e-08)).astype(jnp.bfloat16)
    updates = jnp.einsum(
        "dr,krf->kdf",
        basis,
        whole_of(step, MEMBER, (0, 1), 1).astype(jnp.float32),
        precision=highest,
    )
    return (input_grad, new_first, new_second, updates)


def solution(mesh):
    torus = Mesh(
        mesh.devices.reshape(mesh.shape["group"], 16, 2), ("group", "member_0", "member_1")
    )
    placed = (
        P(GROUP_MEMBER, None),
        P(GROUP_MEMBER, None),
        P(MEMBER, None),
        P(MEMBER, None),
        P(MEMBER, None),
        P(MEMBER, None),
        P(None, MEMBER, None),
        P(None, MEMBER, None),
    )
    return jax.shard_map(
        local,
        mesh=torus,
        in_specs=placed,
        out_specs=(
            P(GROUP_MEMBER, None),
            P(None, MEMBER, None),
            P(None, MEMBER, None),
            P(None, MEMBER, None),
        ),
        check_vma=False,
    )
```

profile of v0, /device:TPU:1, one launch (start us, length us, event | category | flops | bytes accessed | tf_op | source)
XLA Modules:
  0.0 337.4 jit_solution(16014299406178635966)
XLA Ops:
  7.2 1.6 pad_maximum_fusion
  8.9 1.1 broadcast_in_dim.8
  10.0 137.4 %all_to_all.21 = f32[32,64,256]{2,1,0:T(8,128)S(1)} all-to-all(f32[32,64,256]{2,1,0:T(8,128)S(1)} %broadcast_in_dim.8), channel_id=1, replica_groups=mesh['group'=16,'member_0'=16,'member_1'=2] {'member_0','member_1'}, dimensions={0} | all-to-all | bytes 4194304 | tf_op jit(solution)/shard_map/all_to_all | solution.py:31
  147.7 0.8 copy-done.2
  149.1 0.3 fusion.24
  149.8 12.7 %all-gather.3.cloned.1.call-done = bf16[2048,1536]{1,0:T(8,128)(2,1)} async-done(((bf16[64,1536]{1,0:T(8,128)(2,1)}), bf16[2048,1536]{1,0:T(8,128)(2,1)}) %all-gather.3.cloned.1.call-update) | async-done | bytes 6291472 | tf_op jit(solution)/shard_map/all_gather | solution.py:16
  162.4 2.5 fusion.17
  164.9 2.3 fusion.20
  167.3 0.8 multiply_convert_fusion
  169.7 85.5 %all_to_all.22 = f32[32,3,8,512]{3,2,1,0:T(8,128)S(1)} all-to-all(f32[32,3,8,512]{3,2,1,0:T(8,128)S(1)} %maximum_bitcast_fusion), channel_id=1, replica_groups=mesh['group'=16,'member_0'=16,'member_1'=2] {'member_0','member_1'}, dimensions={0} | all-to-all | bytes 3145728 | tf_op jit(solution)/shard_map/all_to_all | solution.py:47
  255.3 1.0 broadcast_in_dim.9
  256.3 6.8 %all-to-all-start.2 = ((f32[16,3,8,512]{3,2,1,0:T(8,128)}), f32[16,3,8,512]{3,2,1,0:T(8,128)S(1)}, u32[]{:S(2)}, u32[]{:S(2)}) async-start(f32[16,3,8,512]{3,2,1,0:T(8,128)} %broadcast_in_dim.9), calls=%async_computation.2 | async-start | bytes 1572864 | tf_op jit(solution)/shard_map/all_to_all | solution.py:31
  263.1 2.4 fusion.4
  265.5 11.0 %all-to-all-done.2 = f32[16,3,8,512]{3,2,1,0:T(8,128)S(1)} async-done(((f32[16,3,8,512]{3,2,1,0:T(8,128)}), f32[16,3,8,512]{3,2,1,0:T(8,128)S(1)}, u32[]{:S(2)}, u32[]{:S(2)}) %all-to-all-start.2) | async-done | bytes 786464 | tf_op jit(solution)/shard_map/all_to_all | solution.py:31
  276.5 0.6 multiply_reduce_fusion
  277.1 1.3 broadcast_in_dim.10
  278.4 5.5 %all-to-all-start.3 = ((f32[32,1,1]{2,1,0:T(1,128)}), f32[32,1,1]{2,1,0:T(1,128)S(1)}, u32[]{:S(2)}, u32[]{:S(2)}) async-start(f32[32,1,1]{2,1,0:T(1,128)} %broadcast_in_dim.10), calls=%async_computation.3 | async-start | bytes 32768 | tf_op jit(solution)/shard_map/all_to_all | solution.py:31
  283.9 3.2 fusion
  287.1 8.6 %all-to-all-done.3 = f32[32,1,1]{2,1,0:T(1,128)S(1)} async-done(((f32[32,1,1]{2,1,0:T(1,128)}), f32[32,1,1]{2,1,0:T(1,128)S(1)}, u32[]{:S(2)}, u32[]{:S(2)}) %all-to-all-start.3) | async-done | bytes 160 | tf_op jit(solution)/shard_map/all_to_all | solution.py:31
  295.8 0.6 reduce_sum.39
  297.1 0.7 divide_convert_fusion
  297.8 21.5 %all-gather = bf16[48,8,512]{2,1,0:T(8,128)(2,1)S(1)} all-gather(bf16[3,8,512]{2,1,0:T(8,128)(2,1)S(1)} %get-tuple-element.4), channel_id=2, replica_groups=mesh['group'=16,'member_0'=16,'member_1'=2] {'member_0'}, dimensions={0}, use_global_device_ids=true | all-gather | bytes 417792 | tf_op jit(solution)/shard_map/all_gather | solution.py:58
  319.2 10.0 %all_gather.11 = bf16[32,3,8,512]{3,2,1,0:T(8,128)(2,1)S(1)} all-gather(bf16[16,3,8,512]{3,2,1,0:T(8,128)(2,1)S(1)} %bitcast.70), channel_id=1, replica_groups=mesh['group'=16,'member_0'=16,'member_1'=2] {'member_1'}, dimensions={0}, use_global_device_ids=true | all-gather | bytes 1179648 | tf_op jit(solution)/shard_map/all_gather | solution.py:58
  329.3 1.3 convolution_bitcast_fusion
  (27 shorter events, 3.2 us)
Async XLA Ops:
  7.2 141.6 %copy-start = (bf16[128,2048]{1,0:T(8,128)(2,1)S(1)}, bf16[128,2048]{1,0:T(8,128)(2,1)}, u32[]{:S(2)}) copy-start(bf16[128,2048]{1,0:T(8,128)(2,1)} %param.8) | copy-start | bytes 1572868
  7.2 155.2 %all-gather.3.cloned.1.call-start = ((), (), s32[]{:S(2)}) async-start(), calls=%async_computation.4 | async-start | bytes 6488064 | tf_op jit(solution)/shard_map/all_gather | solution.py:16
  147.4 1.0 copy-start.2
  162.4 4.8 %copy-start.1 = (bf16[2048,1536]{1,0:T(8,128)(2,1)S(1)}, bf16[2048,1536]{1,0:T(8,128)(2,1)}, u32[]{:S(2)}) copy-start(bf16[2048,1536]{1,0:T(8,128)(2,1)} %all-gather.3.cloned.1.call-done) | copy-start | bytes 18874372
  256.3 20.2 %all-to-all-start.2 = ((f32[16,3,8,512]{3,2,1,0:T(8,128)}), f32[16,3,8,512]{3,2,1,0:T(8,128)S(1)}, u32[]{:S(2)}, u32[]{:S(2)}) async-start(f32[16,3,8,512]{3,2,1,0:T(8,128)} %broadcast_in_dim.9), calls=%async_computation.2 | async-start | bytes 1572864 | tf_op jit(solution)/shard_map/all_to_all | solution.py:31
  276.5 20.6 %copy-start.4 = (f32[3,8,512]{2,1,0:T(8,128)S(1)}, f32[3,8,512]{2,1,0:T(8,128)}, u32[]{:S(2)}) copy-start(f32[3,8,512]{2,1,0:T(8,128)} %param.15) | copy-start | bytes 147460
  276.5 20.6 %copy-start.5 = (f32[3,8,512]{2,1,0:T(8,128)S(1)}, f32[3,8,512]{2,1,0:T(8,128)}, u32[]{:S(2)}) copy-start(f32[3,8,512]{2,1,0:T(8,128)} %param.14) | copy-start | bytes 147460
  278.4 17.3 %all-to-all-start.3 = ((f32[32,1,1]{2,1,0:T(1,128)}), f32[32,1,1]{2,1,0:T(1,128)S(1)}, u32[]{:S(2)}, u32[]{:S(2)}) async-start(f32[32,1,1]{2,1,0:T(1,128)} %broadcast_in_dim.10), calls=%async_computation.3 | async-start | bytes 32768 | tf_op jit(solution)/shard_map/all_to_all | solution.py:31
  287.1 42.2 %copy-start.3 = (f32[64,256]{1,0:T(8,128)S(1)}, f32[64,256]{1,0:T(8,128)}, u32[]{:S(2)}) copy-start(f32[64,256]{1,0:T(8,128)} %param.13) | copy-start | bytes 196612
Sparse Core Ops, SparseCore 0:
  10.7 151.6 all-gather.2
where the time goes:
time: 338 us; the launch traced here: 337 us
  blocking collectives  254 us (75%)
  waiting for transfers between devices  32.3 us (10%)
  matrix products  15.2 us (4%)
  between operations  14.9 us (4%)
  starting transfers between devices  12.3 us (4%)
  local copies, waits for them, and re-layouts  4.19 us (1%)
  other arithmetic  4.12 us (1%)
    all_to_all x1, blocking collectives, copy_for_each(): lax.all_to_all(jnp.broadcast_to(value[None], (peers, *value.shape)), axis...  137 us
    all_to_all x1, blocking collectives, sum_at_owner(): lax.all_to_all(pieces, axis, split_axis=0, concat_axis=0, tiled=True)  85.5 us
    all_gather x2, blocking collectives, gather_in_order(): pieces = lax.all_gather(pieces, axes[k], axis=0, tiled=True)  31.4 us
    all_to_all x2, waiting for transfers between devices, copy_for_each(): lax.all_to_all(jnp.broadcast_to(value[None], (peers, *value.shape)), axis...  19.6 us
    all_gather x1, waiting for transfers between devices, in_one_piece(): lax.all_gather(both, axis, axis=dim, tiled=True)  12.7 us
    all_to_all x2, starting transfers between devices, copy_for_each(): lax.all_to_all(jnp.broadcast_to(value[None], (peers, *value.shape)), axis...  12.3 us
  transfers between devices with their start and end apart: 3, of which 3 were waited for; matrix products, arithmetic and copies ran while one was open for 2% of the time, Pallas kernels for 0%

commit v1 on v0

--- a/solution.py
+++ b/solution.py
@@ -9,6 +9,14 @@
 RANK = 256
 MEMBER = ("member_0", "member_1")
 GROUP_MEMBER = ("group", "member_0", "member_1")
+
+
+def wait_sites(local_block, mesh_ax):
+    chunks = []
+    for _ in range(jax.lax.axis_size(mesh_ax)):
+        chunks.append(local_block)
+    y = jnp.concatenate(jax.lax.all_to_all(jnp.stack(chunks), mesh_ax, 0, 0), axis=0)
+    return y
 
 
 def in_one_piece(arrays, axis, dim, along):
@@ -55,7 +63,7 @@
 def gather_in_order(value, axes, order):
     pieces = value[None]
     for k in order:
-        pieces = lax.all_gather(pieces, axes[k], axis=0, tiled=True)
+        pieces = wait_sites(pieces, axes[k])
     block = [lax.axis_size(axes[k]) for k in reversed(order)]
     pieces = pieces.reshape(*block, *value.shape)
     turned = sorted(range(len(order)), key=lambda place: order[len(order) - 1 - place])

time: 338 us -> 337 us (level)
  blocking collectives: 254 us -> 270 us
  starting transfers between devices: 12.3 us -> 3.59 us
  waiting for transfers between devices: 32.3 us -> 24.9 us
    all_to_all x1 -> x3, blocking collectives: 137 us -> 174 us  [copy_for_each(): lax.all_to_all(jnp.broadcast_to(value[None], (peers, *value.shape)), axis...]
    all_gather x2 -> x0, blocking collectives: 31.4 us -> none  [gather_in_order(): pieces = lax.all_gather(pieces, axes[k], axis=0, tiled=True)]
    all_to_all x0 -> x1, blocking collectives: none -> 10.9 us  [wait_sites(): jax.lax.all_to_all(jnp.stack(chunks), mesh_ax, 0, 0)]
    all_to_all x2 -> x1, starting transfers between devices: 12.3 us -> 3.55 us  [wait_sites(): jax.lax.all_to_all(jnp.stack(chunks), mesh_ax, 0, 0)]
    all_to_all x2 -> x1, waiting for transfers between devices: 19.6 us -> 12.3 us  [wait_sites(): jax.lax.all_to_all(jnp.stack(chunks), mesh_ax, 0, 0)]
  transfers between devices with their start and end apart: 3 -> 2, of which waited for: 3 -> 2; matrix products, arithmetic and copies ran while one was open for 2% -> 2% of each run, Pallas kernels for 0% -> 0%
where the time goes in v1:
time: 337 us
  blocking collectives  270 us (80%)
  waiting for transfers between devices  24.9 us (7%)
  matrix products  15.2 us (5%)
  between operations  14.9 us (4%)
  other arithmetic  4.17 us (1%)
  starting transfers between devices  3.59 us (1%)
  local copies, waits for them, and re-layouts  3.52 us (1%)
    all_to_all x3, blocking collectives, copy_for_each(): lax.all_to_all(jnp.broadcast_to(value[None], (peers, *value.shape)), axis...  174 us
    all_to_all x1, blocking collectives, sum_at_owner(): lax.all_to_all(pieces, axis, split_axis=0, concat_axis=0, tiled=True)  85.5 us
    all_gather x1, waiting for transfers between devices, in_one_piece(): lax.all_gather(both, axis, axis=dim, tiled=True)  12.7 us
    all_to_all x1, waiting for transfers between devices, wait_sites(): jax.lax.all_to_all(jnp.stack(chunks), mesh_ax, 0, 0)  12.3 us
    all_to_all x1, blocking collectives, wait_sites(): jax.lax.all_to_all(jnp.stack(chunks), mesh_ax, 0, 0)  10.9 us
  transfers between devices with their start and end apart: 2, of which 2 were waited for; matrix products, arithmetic and copies ran while one was open for 2% of the time, Pallas kernels for 0%

profile of v1, /device:TPU:1, one launch (start us, length us, event | category | flops | bytes accessed | tf_op | source)
XLA Modules:
  0.0 336.6 jit_solution(4547234676168937089)
XLA Ops:
  7.2 1.6 pad_maximum_fusion.1
  8.9 1.1 broadcast_in_dim.6
  10.0 137.4 %all_to_all.31 = f32[32,64,256]{2,1,0:T(8,128)S(1)} all-to-all(f32[32,64,256]{2,1,0:T(8,128)S(1)} %broadcast_in_dim.6), channel_id=1, replica_groups=mesh['group'=16,'member_0'=16,'member_1'=2] {'member_0','member_1'}, dimensions={0} | all-to-all | bytes 4194304 | tf_op jit(solution)/shard_map/all_to_all | solution.py:39
  147.7 0.8 copy-done.2
  149.1 0.3 fusion.24
  149.4 0.3 fusion.23
  149.8 12.7 %all-gather.2.cloned.1.call-done = bf16[2048,1536]{1,0:T(8,128)(2,1)} async-done(((bf16[64,1536]{1,0:T(8,128)(2,1)}), bf16[2048,1536]{1,0:T(8,128)(2,1)}) %all-gather.2.cloned.1.call-update) | async-done | bytes 6291472 | tf_op jit(solution)/shard_map/all_gather | solution.py:24
  162.4 2.5 fusion.17
  164.9 2.3 fusion.20
  167.3 0.8 multiply_convert_fusion
  169.7 85.5 %all_to_all.32 = f32[32,3,8,512]{3,2,1,0:T(8,128)S(1)} all-to-all(f32[32,3,8,512]{3,2,1,0:T(8,128)S(1)} %maximum_bitcast_fusion), channel_id=1, replica_groups=mesh['group'=16,'member_0'=16,'member_1'=2] {'member_0','member_1'}, dimensions={0} | all-to-all | bytes 3145728 | tf_op jit(solution)/shard_map/all_to_all | solution.py:55
  255.4 20.2 %all_to_all.33 = f32[16,3,8,512]{3,2,1,0:T(8,128)S(1)} all-to-all(f32[16,3,8,512]{3,2,1,0:T(8,128)S(1)} %broadcast_in_dim.7), channel_id=1, replica_groups=mesh['group'=16,'member_0'=16,'member_1'=2] {'group'}, dimensions={0} | all-to-all | bytes 1572864 | tf_op jit(solution)/shard_map/all_to_all | solution.py:39
  275.7 0.6 multiply_reduce_fusion
  276.3 0.7 broadcast_in_dim.8
  277.0 16.1 %all_to_all.34 = f32[32,1,1]{2,1,0:T(1,128)S(1)} all-to-all(f32[32,1,1]{2,1,0:T(1,128)S(1)} %broadcast_in_dim.8), channel_id=1, replica_groups=mesh['group'=16,'member_0'=16,'member_1'=2] {'member_0','member_1'}, dimensions={0} | all-to-all | bytes 256 | tf_op jit(solution)/shard_map/all_to_all | solution.py:39
  293.1 0.6 reduce_sum.39
  294.5 0.7 divide_convert_fusion
  295.1 0.8 stack.22
  295.9 3.6 %all-to-all-start.4 = ((bf16[16,1,3,8,512]{4,3,2,1,0:T(8,128)(2,1)}), bf16[16,1,3,8,512]{4,3,2,1,0:T(8,128)(2,1)S(1)}, u32[]{:S(2)}, u32[]{:S(2)}) async-start(bf16[16,1,3,8,512]{4,3,2,1,0:T(8,128)(2,1)} %stack.22), calls=%async_computation.4 | async-start | bytes 786432 | tf_op jit(solution)/shard_map/all_to_all | solution.py:18
  299.5 2.4 fusion.4
  301.9 3.2 fusion
  305.1 12.3 %all-to-all-done.4 = bf16[16,1,3,8,512]{4,3,2,1,0:T(8,128)(2,1)S(1)} async-done(((bf16[16,1,3,8,512]{4,3,2,1,0:T(8,128)(2,1)}), bf16[16,1,3,8,512]{4,3,2,1,0:T(8,128)(2,1)S(1)}, u32[]{:S(2)}, u32[]{:S(2)}) %all-to-all-start.4) | async-done | bytes 393248 | tf_op jit(solution)/shard_map/all_to_all | solution.py:18
  317.5 10.9 %all_to_all.35 = bf16[2,16,3,8,512]{4,3,1,2,0:T(8,128)(2,1)S(1)} all-to-all(bf16[2,16,3,8,512]{4,3,1,2,0:T(8,128)(2,1)S(1)} %copy.42), channel_id=1, replica_groups=mesh['group'=16,'member_0'=16,'member_1'=2] {'member_1'}, dimensions={0} | all-to-all | bytes 1572864 | tf_op jit(solution)/shard_map/all_to_all | solution.py:18
  328.5 1.3 convolution_bitcast_fusion
  (29 shorter events, 3.0 us)
Async XLA Ops:
  7.2 141.6 %copy-start = (bf16[128,2048]{1,0:T(8,128)(2,1)S(1)}, bf16[128,2048]{1,0:T(8,128)(2,1)}, u32[]{:S(2)}) copy-start(bf16[128,2048]{1,0:T(8,128)(2,1)} %param.8) | copy-start | bytes 1572868
  7.2 155.2 %all-gather.2.cloned.1.call-start = ((), (), s32[]{:S(2)}) async-start(), calls=%async_computation.6 | async-start | bytes 6488064 | tf_op jit(solution)/shard_map/all_gather | solution.py:24
  147.4 1.0 copy-start.2
  162.4 4.8 %copy-start.1 = (bf16[2048,1536]{1,0:T(8,128)(2,1)S(1)}, bf16[2048,1536]{1,0:T(8,128)(2,1)}, u32[]{:S(2)}) copy-start(bf16[2048,1536]{1,0:T(8,128)(2,1)} %all-gather.2.cloned.1.call-done) | copy-start | bytes 18874372
  255.2 39.2 %copy-start.4 = (f32[3,8,512]{2,1,0:T(8,128)S(1)}, f32[3,8,512]{2,1,0:T(8,128)}, u32[]{:S(2)}) copy-start(f32[3,8,512]{2,1,0:T(8,128)} %param.15) | copy-start | bytes 147460
  255.2 39.2 %copy-start.5 = (f32[3,8,512]{2,1,0:T(8,128)S(1)}, f32[3,8,512]{2,1,0:T(8,128)}, u32[]{:S(2)}) copy-start(f32[3,8,512]{2,1,0:T(8,128)} %param.14) | copy-start | bytes 147460
  295.9 21.5 %all-to-all-start.4 = ((bf16[16,1,3,8,512]{4,3,2,1,0:T(8,128)(2,1)}), bf16[16,1,3,8,512]{4,3,2,1,0:T(8,128)(2,1)S(1)}, u32[]{:S(2)}, u32[]{:S(2)}) async-start(bf16[16,1,3,8,512]{4,3,2,1,0:T(8,128)(2,1)} %stack.22), calls=%async_computation.4 | async-start | bytes 786432 | tf_op jit(solution)/shard_map/all_to_all | solution.py:18
  317.5 11.0 %copy-start.3 = (f32[64,256]{1,0:T(8,128)S(1)}, f32[64,256]{1,0:T(8,128)}, u32[]{:S(2)}) copy-start(f32[64,256]{1,0:T(8,128)} %param.13) | copy-start | bytes 196612
Sparse Core Ops, SparseCore 0:
  10.7 151.6 all-gather.1
